TPU v7x, 32 devices: a whole 2x2x4 slice. The times are simulated.
32 devices in a mesh: dp: 8 (over z, y), fsdp: 4 (over x, core).
Axes of the slice: x: 2, y: 2, z: 4, core: 2. Of those that a mesh axis runs over, the one named last changes fastest.
Arguments:
- tokens: bfloat16 [16384, 768], P(('dp', 'fsdp')), may hold values from -6 to 6
- valid_mask: int32 [16384], P(('dp', 'fsdp')), may hold values 0 or 1
- target: bfloat16 [16384, 768], P(('dp', 'fsdp')), may hold values from -8 to 8
- params: float32 [55552, 128], P(('dp', 'fsdp')), may hold values from -4 to 4, as said below
- first_moment: float32 [55552, 128], P(('dp', 'fsdp')), may hold values from -1 to 1, as said below
- second_moment: float32 [55552, 128], P(('dp', 'fsdp')), may hold values from 0 to 1, as said below
Outputs:
- activations: bfloat16 [16384, 768], P(('dp', 'fsdp'))
- loss: float32 [], replicated
- input_grad: float32 [16384, 768], P(('dp', 'fsdp'))
- new_params: float32 [55552, 128], P(('dp', 'fsdp'))
- new_first: float32 [55552, 128], P(('dp', 'fsdp'))
- new_second: float32 [55552, 128], P(('dp', 'fsdp'))
Inputs may be any that keep to these rules, and one draw needn't show every extreme that they name: `params`: entries beyond 7087104 in row order are zero. `first_moment`: entries beyond 7087104 in row order are zero. `second_moment`: entries beyond 7087104 in row order are zero.
All inputs are finite; a program needn't handle non-finite values. No bound on the sum of `valid_mask` on one device may be relied on, other than what follows from the above.
Results may differ from a plain program's by a relative error of at most 0.012.
The roundings to bfloat16 on the way count: a program that leaves them out, or rounds other values in their place, can miss the bound.
Values may be sent and summed in bfloat16 or wider, within the bound.
A program may use at most 128 MiB of HBM per device.

v0:
```python
import jax
import jax.numpy as jnp
from jax import lax
from jax.sharding import PartitionSpec as P

D = 768
HEADS = 12
HEAD = 64
FF = 3072
FRAMES = 16
STEP = 10


norm_epsilon = 1e-06
adam_epsilon = 1e-08
beta_one = 0.9
beta_two = 0.999
learn_rate = 0.1
weight_decay = 0.05


def unpack(tiled):
    flat = tiled.reshape(-1)
    layout = [(D, 3 * D), (D, D), (D, FF), (D, FF)]
    pieces = []
    offset = 0
    for height, breadth in layout:
        pieces.append(flat[offset : offset + height * breadth].reshape(height, breadth))
        offset = offset + height * breadth
    for length in [D] * 8 + [FF]:
        pieces.append(flat[offset : offset + length].astype(jnp.float32))
        offset = offset + length
    return pieces


def layer_norm(values, gain, shift):
    center = values - jnp.mean(values, -1, keepdims=True)
    spread = jnp.mean(center * center, -1, keepdims=True)
    return center * lax.rsqrt(spread + norm_epsilon) * gain + shift


def exact_gelu(values):
    return jax.nn.gelu(values, approximate=False)


def collect(shard):
    lowered = shard.astype(jnp.bfloat16)
    whole = lax.all_gather(lowered, ("dp", "fsdp"), axis=0, tiled=True)
    return whole


def reduce_rows(full):
    summed = lax.psum_scatter(full, ("dp", "fsdp"), scatter_dimension=0, tiled=True)
    return summed


def contract_rows(left, right):
    return lax.dot_general(
        left, right, (((0,), (0,)), ((), ())), preferred_element_type=jnp.float32
    )


def contract_cols(left, right):
    return lax.dot_general(
        left, right, (((1,), (1,)), ((), ())), preferred_element_type=jnp.float32
    )


def column_sum(values):
    return jnp.sum(values.astype(jnp.float32), 0)


def shards(tokens, valid_mask, target, params, first_moment, second_moment):
    token_rows = tokens.shape[0]
    places = token_rows // FRAMES
    devices = lax.axis_size("dp") * lax.axis_size("fsdp")
    lane_count = params.shape[1]
    total_rows = params.shape[0] * devices
    score_scale = HEAD ** (-0.5)
    mask_values = valid_mask.astype(jnp.float32)
    gathered = collect(params)
    (
        w_qkv,
        w_proj,
        w_in,
        w_out,
        gain_one,
        shift_one,
        bias_query,
        bias_value,
        bias_proj,
        gain_two,
        shift_two,
        bias_out,
        bias_in,
    ) = unpack(gathered)
    inputs = tokens.astype(jnp.float32)
    normed_low = layer_norm(inputs, gain_one, shift_one).astype(jnp.bfloat16)
    bias_all = jnp.concatenate([bias_query, jnp.zeros_like(bias_query), bias_value])
    mixed_low = (jnp.dot(normed_low, w_qkv, preferred_element_type=jnp.float32) + bias_all).astype(
        jnp.bfloat16
    )
    heads_view = mixed_low.reshape(places, FRAMES, 3, HEADS, HEAD)
    queries = heads_view[:, :, 0]
    key_part = heads_view[:, :, 1]
    values = heads_view[:, :, 2]
    scores = (
        jnp.einsum("pfhe,pghe->phfg", queries, key_part, preferred_element_type=jnp.float32)
        * score_scale
    )
    row_max = jnp.max(scores, -1, keepdims=True)
    log_total = row_max + jnp.log(jnp.sum(jnp.exp(scores - row_max), -1, keepdims=True))
    probs = jnp.exp(scores - log_total)
    probs_low = probs.astype(jnp.bfloat16)
    attended = jnp.einsum("phfg,pghe->pfhe", probs_low, values, preferred_element_type=jnp.float32)
    attended_low = attended.reshape(token_rows, D).astype(jnp.bfloat16)
    branch = jnp.dot(attended_low, w_proj, preferred_element_type=jnp.float32) + bias_proj
    middle = inputs + branch
    normed_two_low = layer_norm(middle, gain_two, shift_two).astype(jnp.bfloat16)
    hidden = jnp.dot(normed_two_low, w_in, preferred_element_type=jnp.float32) + bias_in
    active_low = exact_gelu(hidden).astype(jnp.bfloat16)
    second_branch = contract_cols(active_low, w_out) + bias_out
    output = middle + second_branch
    misfit = output - target.astype(jnp.float32)
    squares = jnp.sum(mask_values * jnp.sum(misfit * misfit, -1))
    total_error, kept_count = lax.psum((squares, jnp.sum(mask_values)), ("dp", "fsdp"))
    denominator = kept_count * D
    grad_out = 2.0 / denominator * mask_values[:, None] * misfit
    regathered = collect(params)
    w_qkv, w_proj, w_in, w_out = unpack(regathered)[:4]
    grad_out_low = grad_out.astype(jnp.bfloat16)
    grad_bias_out = column_sum(grad_out_low)
    grad_w_out = contract_rows(grad_out_low, active_low)
    grad_active = jnp.dot(grad_out_low, w_out, preferred_element_type=jnp.float32)
    gelu_value, gelu_pull = jax.vjp(exact_gelu, hidden)
    grad_hidden_low = gelu_pull(grad_active)[0].astype(jnp.bfloat16)
    grad_bias_in = column_sum(grad_hidden_low)
    grad_w_in = contract_rows(normed_two_low, grad_hidden_low)
    grad_normed_two = contract_cols(grad_hidden_low, w_in)
    norm_value, second_pull = jax.vjp(layer_norm, middle, gain_two, shift_two)
    grad_middle_norm, grad_gain_two, grad_shift_two = second_pull(grad_normed_two)
    grad_middle = grad_out + grad_middle_norm
    grad_branch_low = grad_middle.astype(jnp.bfloat16)
    grad_bias_proj = column_sum(grad_branch_low)
    grad_w_proj = contract_rows(attended_low, grad_branch_low)
    grad_attended_low = (
        contract_cols(grad_branch_low, w_proj)
        .astype(jnp.bfloat16)
        .reshape(places, FRAMES, HEADS, HEAD)
    )
    grad_values = jnp.einsum(
        "phfg,pfhe->pghe", probs_low, grad_attended_low, preferred_element_type=jnp.float32
    )
    grad_probs = jnp.einsum(
        "pfhe,pghe->phfg", grad_attended_low, values, preferred_element_type=jnp.float32
    )
    grad_scores_low = (
        probs * (grad_probs - jnp.sum(probs * grad_probs, -1, keepdims=True))
    ).astype(jnp.bfloat16)
    grad_queries = (
        jnp.einsum("phfg,pghe->pfhe", grad_scores_low, key_part, preferred_element_type=jnp.float32)
        * score_scale
    )
    grad_keys = (
        jnp.einsum("phfg,pfhe->pghe", grad_scores_low, queries, preferred_element_type=jnp.float32)
        * score_scale
    )
    grad_mixed_low = (
        jnp.stack([grad_queries, grad_keys, grad_values], 2)
        .reshape(token_rows, 3 * D)
        .astype(jnp.bfloat16)
    )
    grad_bias_query = column_sum(grad_mixed_low[:, :D])
    grad_bias_value = column_sum(grad_mixed_low[:, 2 * D :])
    grad_w_qkv = contract_rows(normed_low, grad_mixed_low)
    grad_normed_one = contract_cols(grad_mixed_low, w_qkv)
    first_value, first_pull = jax.vjp(layer_norm, inputs, gain_one, shift_one)
    grad_inputs_norm, grad_gain_one, grad_shift_one = first_pull(grad_normed_one)
    grad_inputs = grad_middle + grad_inputs_norm
    used_grad = jnp.concatenate(
        [
            grad_w_qkv.reshape(-1),
            grad_w_proj.reshape(-1),
            grad_w_in.reshape(-1),
            grad_w_out.reshape(-1),
            grad_gain_one,
            grad_shift_one,
            grad_bias_query,
            grad_bias_value,
            grad_bias_proj,
            grad_gain_two,
            grad_shift_two,
            grad_bias_out,
            grad_bias_in,
        ]
    )
    padding = jnp.zeros((total_rows * lane_count - used_grad.shape[0],), jnp.float32)
    whole_grad = jnp.concatenate([used_grad, padding]).reshape(total_rows, lane_count)
    gradient = reduce_rows(whole_grad)
    loss = total_error / denominator
    new_first = beta_one * first_moment + (1.0 - beta_one) * gradient
    new_second = beta_two * second_moment + (1.0 - beta_two) * gradient * gradient
    first_hat = new_first / (1.0 - beta_one**STEP)
    second_hat = new_second / (1.0 - beta_two**STEP)
    new_params = params - learn_rate * (
        first_hat / (jnp.sqrt(second_hat) + adam_epsilon) + weight_decay * params
    )
    input_grad = grad_inputs * float(token_rows * devices * D)
    return (output.astype(jnp.bfloat16), loss, input_grad, new_params, new_first, new_second)


def solution(mesh):
    return jax.shard_map(
        shards,
        mesh=mesh,
        in_specs=(
            P(("dp", "fsdp"), None),
            P(("dp", "fsdp")),
            P(("dp", "fsdp"), None),
            P(("dp", "fsdp"), None),
            P(("dp", "fsdp"), None),
            P(("dp", "fsdp"), None),
        ),
        out_specs=(
            P(("dp", "fsdp"), None),
            P(),
            P(("dp", "fsdp"), None),
            P(("dp", "fsdp"), None),
            P(("dp", "fsdp"), None),
            P(("dp", "fsdp"), None),
        ),
        check_vma=False,
    )
```

profile of v0, /device:TPU:30, one launch (start us, length us, event | category | flops | bytes accessed | tf_op | source)
XLA Modules:
  0.0 705.1 jit_solution(17554476589164988421)
XLA Ops:
  12.1 100.6 %all-gather.2.cloned.1.call-done = bf16[55552,128]{1,0:T(8,128)(2,1)} async-done(((bf16[1736,128]{1,0:T(8,128)(2,1)}), bf16[55552,128]{1,0:T(8,128)(2,1)}) %all-gather.2.cloned.1.call-update) | async-done | bytes 14221328 | tf_op jit(solution)/shard_map/all_gather | solution.py:48
  114.7 5.2 reshape.206
  120.7 4.4 fusion.6
  125.1 6.0 reshape.207
  131.1 5.0 fusion.53
  142.0 3.9 convert_element_type.182
  148.3 3.3 reshape.208
  155.7 8.3 %fusion.52 = (bf16[18432,128]{1,0:T(8,128)(2,1)}, bf16[18432,128]{1,0:T(8,128)(2,1)}) fusion(bf16[55552,128]{1,0:T(8,128)(2,1)} %all-gather.2.cloned.1.call-done), kind=kLoop, calls=%fused_computation.133 | loop fusion | bytes 18874368 | tf_op jit(solution)/shard_map/slice | solution.py:28
  164.0 8.2 %reshape.209 = bf16[768,3072]{1,0:T(8,128)(2,1)} reshape(bf16[18432,128]{1,0:T(8,128)(2,1)} %get-tuple-element.41) | data formatting | bytes 9437184 | tf_op jit(solution)/shard_map/reshape | solution.py:28
  172.2 8.2 %reshape.210 = bf16[768,3072]{1,0:T(8,128)(2,1)} reshape(bf16[18432,128]{1,0:T(8,128)(2,1)} %get-tuple-element.40) | data formatting | bytes 9437184 | tf_op jit(solution)/shard_map/reshape | solution.py:28
  181.1 20.9 %multiply_convert_fusion = (bf16[512,3072]{1,0:T(8,128)(2,1)S(1)}, f32[512,3072]{1,0:T(8,128)}, f32[512,3072]{1,0:T(8,128)}) fusion(f32[3072]{0:T(1024)S(1)} %fusion.27, bf16[768,3072]{1,0:T(8,128)(2,1)} %reshape.209, f32[512,768]{1,0:T(8,128)} %copy-done.13, f32[768]{0:T(1024)S(1)} %get-tuple-element.33, f32[768]{0:T(1024)S(1)} %get-tuple-element.34, ...), kind=kOutput, calls=%fused_computation.5 | convolution fusion | flops 2521694208 | bytes 22042624 | tf_op jit(solution)/shard_map/dot_general | solution.py:120
  202.1 3.9 multiply_reduce_fusion.4
  206.6 41.6 %all-reduce.1 = (f32[]{:T(128)}, f32[]{:T(128)}) all-reduce(f32[]{:T(128)} %get-tuple-element.16, f32[]{:T(128)} %get-tuple-element.15), channel_id=1, replica_groups=mesh['dp'=8,'fsdp'=4] {'dp','fsdp'}, use_global_device_ids=true, to_apply=%region_8.0 | all-reduce | flops 2 | bytes 16 | tf_op jit(solution)/shard_map/psum | solution.py:126
  250.9 9.3 %convert_reduce_fusion = (f32[3072]{0:T(1024)S(1)}, bf16[512,3072]{1,0:T(8,128)(2,1)S(1)}) fusion(f32[512,3072]{1,0:T(8,128)} %get-tuple-element.31, f32[512,3072]{1,0:T(8,128)} %get-tuple-element.50, f32[3072]{0:T(1024)S(1)} %fusion.27, bf16[512,768]{1,0:T(8,128)(2,1)S(1)} %get-tuple-element.25, bf16[768,3072]{1,0:T(8,128)(2,1)} %reshape.210), kind=kOutput, calls=%fused_computation.3 | convolution fusion | flops 2442654720 | bytes 21258240 | tf_op jit(solution)/shard_map/dot_general | solution.py:134
  260.3 3.0 multiply_reduce_fusion.2
  269.1 4.2 reshape.211
  283.0 4.3 copy.36
  287.3 7.5 %convert_element_type.204 = bf16[512,2304]{1,0:T(8,128)(2,1)S(1)} reshape(bf16[32,16,3,12,64]{4,3,2,1,0:T(8,128)(2,1)} %copy.36) | data formatting | bytes 4718592 | tf_op jit(solution)/shard_map/convert_element_type | solution.py:171
  296.2 5.2 fusion.48
  301.4 6.9 fusion.43
  311.6 5.5 convolution_bitcast_fusion.1
  317.1 5.0 convolution_bitcast_fusion
  322.4 7.9 %reshape.212 = f32[1769472]{0:T(1024)} reshape(f32[768,2304]{1,0:T(8,128)} %fusion.43) | data formatting | bytes 14155776 | tf_op jit(solution)/shard_map/reshape | solution.py:182
  330.3 5.1 constant_dynamic-update-slice_fusion.12
  335.4 3.5 reshape.213
  339.0 9.6 %copy.42 = f32[96,24,8,128]{3,1,2,0:T(8,128)} copy(f32[96,24,8,128]{3,2,1,0:T(8,128)} %convolution_bitcast_fusion.1) | data formatting | bytes 18874368
  348.6 5.9 copy.43
  357.8 9.6 %constant_dynamic-update-slice_fusion.10 = f32[7110656]{0:T(1024)} fusion(f32[7110656]{0:T(1024)} %constant_dynamic-update-slice_fusion.11, f32[2359296]{0:T(1024)} %bitcast.110), kind=kLoop, calls=%fused_computation.91 | loop fusion | bytes 18874368
  367.4 4.0 constant_dynamic-update-slice_fusion.9
  383.7 3.1 add_multiply_fusion
  386.8 306.4 %reduce-scatter.5.cloned.1.call-done = f32[1736,128]{1,0:T(8,128)} async-done(((f32[55552,128]{1,0:T(8,128)}), f32[1736,128]{1,0:T(8,128)}) %reduce-scatter.5.cloned.1.call-update) | async-done | bytes 888848
  693.2 3.6 multiply_subtract_fusion
  (138 shorter events, 58.6 us)
Async XLA Ops:
  7.2 105.5 %all-gather.2.cloned.1.call-start = ((), (), s32[]{:S(2)}) async-start(), calls=%async_computation.1 | async-start | bytes 14665728 | tf_op jit(solution)/shard_map/all_gather | solution.py:48
  9.2 684.0 %reduce-scatter.5.cloned.1.call-start = ((), (), s32[]{:S(2)}) async-start(), calls=%async_computation.2 | async-start | bytes 29331456
  136.1 3.1 copy-start.3
  181.1 21.0 %copy-start.14 = (f32[512,768]{1,0:T(8,128)S(1)}, f32[512,768]{1,0:T(8,128)}, u32[]{:S(2)}) copy-start(f32[512,768]{1,0:T(8,128)} %copy-done.13) | copy-start | bytes 4718596
  181.1 21.0 %copy-start.19 = (bf16[768,3072]{1,0:T(8,128)(2,1)S(1)}, bf16[768,3072]{1,0:T(8,128)(2,1)}, u32[]{:S(2)}) copy-start(bf16[768,3072]{1,0:T(8,128)(2,1)} %reshape.210) | copy-start | bytes 14155780
  181.1 21.0 %copy-start.21 = (bf16[512,768]{1,0:T(8,128)(2,1)S(1)}, bf16[512,768]{1,0:T(8,128)(2,1)}, u32[]{:S(2)}) copy-start(bf16[512,768]{1,0:T(8,128)(2,1)} %param.8) | copy-start | bytes 2359300
  202.1 3.9 copy-start.26
  202.1 3.9 copy-start.29
  248.9 11.4 %slice-start.7 = ((s8[4718592]{0:T(1024)(128)(4,1)}), s8[4194304]{0:T(1024)(128)(4,1)S(1)}, s32[]{:S(2)}) async-start(s8[4718592]{0:T(1024)(128)(4,1)} %bitcast.111), calls=%async_computation.10 | async-start | bytes 8388608
  250.9 9.3 %copy-start.24 = (bf16[512,768]{1,0:T(8,128)(2,1)}, bf16[512,768]{1,0:T(8,128)(2,1)S(1)}, u32[]{:S(2)}) copy-start(bf16[512,768]{1,0:T(8,128)(2,1)S(1)} %get-tuple-element.25) | copy-start | bytes 2359300
  250.9 9.3 %copy-start.15 = (f32[512,768]{1,0:T(8,128)S(1)}, f32[512,768]{1,0:T(8,128)}, u32[]{:S(2)}) copy-start(f32[512,768]{1,0:T(8,128)} %copy-done.13) | copy-start | bytes 4718596
  250.9 9.3 %slice-start.8 = ((s8[4718592]{0:T(1024)(128)(4,1)}), s8[524288]{0:T(1024)(128)(4,1)S(1)}, s32[]{:S(2)}) async-start(s8[4718592]{0:T(1024)(128)(4,1)} %bitcast.111), calls=%async_computation.11 | async-start | bytes 1048576
  260.2 3.0 copy-start.30
  264.9 2.5 copy-start.28
  273.3 2.7 copy-start.2
  273.3 2.8 copy-start.4
  287.3 8.9 %copy-start.9 = (bf16[512,768]{1,0:T(8,128)(2,1)S(1)}, bf16[512,768]{1,0:T(8,128)(2,1)}, u32[]{:S(2)}) copy-start(bf16[512,768]{1,0:T(8,128)(2,1)} %param.6) | copy-start | bytes 2359300
  301.4 6.9 copy-start.1
  301.4 6.9 copy-start.23
  308.4 2.2 copy-start.16
  308.4 3.2 copy-start.31
  311.6 5.5 copy-start.25
  311.6 5.5 copy-start.27
  317.1 5.0 copy-start.12
  335.4 13.2 %slice-start = ((s8[9437184]{0:T(1024)(128)(4,1)}), s8[1048576]{0:T(1024)(128)(4,1)S(1)}, s32[]{:S(2)}) async-start(s8[9437184]{0:T(1024)(128)(4,1)} %bitcast.105), calls=%async_computation.3 | async-start | bytes 2097152
  338.9 9.6 %slice-start.1 = ((s8[9437184]{0:T(1024)(128)(4,1)}), s8[4194304]{0:T(1024)(128)(4,1)S(1)}, s32[]{:S(2)}) async-start(s8[9437184]{0:T(1024)(128)(4,1)} %bitcast.105), calls=%async_computation.4 | async-start | bytes 8388608
  339.0 9.6 %slice-start.2 = ((s8[9437184]{0:T(1024)(128)(4,1)}), s8[4194304]{0:T(1024)(128)(4,1)S(1)}, s32[]{:S(2)}) async-start(s8[9437184]{0:T(1024)(128)(4,1)} %bitcast.105), calls=%async_computation.5 | async-start | bytes 8388608
  348.6 5.9 copy-start.17
  356.1 11.2 %slice-start.3 = ((s8[9437184]{0:T(1024)(128)(4,1)}), s8[4194304]{0:T(1024)(128)(4,1)S(1)}, s32[]{:S(2)}) async-start(s8[9437184]{0:T(1024)(128)(4,1)} %bitcast.107), calls=%async_computation.6 | async-start | bytes 8388608
  357.8 9.6 %slice-start.4 = ((s8[9437184]{0:T(1024)(128)(4,1)}), s8[4194304]{0:T(1024)(128)(4,1)S(1)}, s32[]{:S(2)}) async-start(s8[9437184]{0:T(1024)(128)(4,1)} %bitcast.107), calls=%async_computation.7 | async-start | bytes 8388608
  357.8 9.6 %slice-start.5 = ((s8[9437184]{0:T(1024)(128)(4,1)}), s8[1048576]{0:T(1024)(128)(4,1)S(1)}, s32[]{:S(2)}) async-start(s8[9437184]{0:T(1024)(128)(4,1)} %bitcast.107), calls=%async_computation.8 | async-start | bytes 2097152
  383.0 310.3 %copy-start.20 = (f32[1736,128]{1,0:T(8,128)S(1)}, f32[1736,128]{1,0:T(8,128)}, u32[]{:S(2)}) copy-start(f32[1736,128]{1,0:T(8,128)} %param.9) | copy-start | bytes 2666500
  (11 other events, 16.9 us)
Sparse Core Ops, SparseCore 0:
  11.4 101.2 all-gather.1
  383.1 310.1 reduce-scatter.4
where the time goes:
time: 716 us; the launch traced here: 705 us
  waiting for transfers between devices  407 us (57%)
  local copies, waits for them, and re-layouts  138 us (19%)
  matrix products  78.8 us (11%)
  blocking collectives  41.6 us (6%)
  other arithmetic  22.5 us (3%)
  between operations  17.3 us (2%)
    unnamed x3, waiting for transfers between devices  306 us
    all_gather x1, waiting for transfers between devices, collect(): whole = lax.all_gather(lowered, ('dp', 'fsdp'), axis=0, tiled=True)  101 us
    unnamed x95, local copies, waits for them, and re-layouts  55.3 us
    psum x1, blocking collectives, shards(): lax.psum((squares, jnp.sum(mask_values)), ('dp', 'fsdp'))  41.6 us
    reshape x4, local copies, waits for them, and re-layouts, unpack(): flat[offset:offset + height * breadth].reshape(height, breadth)  24.9 us
    dot_general x1, matrix products, shards(): jnp.dot(normed_two_low, w_in, preferred_element_type=jnp.float32) + bias_in  20.9 us
    dot_general x4, matrix products, contract_rows(): lax.dot_general(left, right, (((0,), (0,)), ((), ())), preferred_element_...  19.6 us
  transfers between devices with their start and end apart: 2, of which 2 were waited for; matrix products, arithmetic and copies ran while one was open for 1% of the time, Pallas kernels for 0%

commit v1 on v0

--- a/solution.py
+++ b/solution.py
@@ -50,8 +50,10 @@
 
 
 def reduce_rows(full):
-    summed = lax.psum_scatter(full, ("dp", "fsdp"), scatter_dimension=0, tiled=True)
-    return summed
+    summed = lax.psum_scatter(
+        full.astype(jnp.bfloat16), ("dp", "fsdp"), scatter_dimension=0, tiled=True
+    )
+    return summed.astype(jnp.float32)
 
 
 def contract_rows(left, right):

time: 716 us -> 565 us (0.79)
  the two profiles are of different devices: /device:TPU:30 before, /device:TPU:0 now
where the time goes in v1:
time: 565 us; the launch traced here: 555 us
  waiting for transfers between devices  285 us (50%)
  local copies, waits for them, and re-layouts  110 us (19%)
  matrix products  80.6 us (14%)
  blocking collectives  39 us (7%)
  other arithmetic  23.2 us (4%)
  between operations  17.6 us (3%)
    unnamed x3, waiting for transfers between devices  180 us
    all_gather x1, waiting for transfers between devices, collect(): whole = lax.all_gather(lowered, ('dp', 'fsdp'), axis=0, tiled=True)  105 us
    psum x1, blocking collectives, shards(): lax.psum((squares, jnp.sum(mask_values)), ('dp', 'fsdp'))  39 us
    unnamed x105, local copies, waits for them, and re-layouts  33.1 us
    reshape x4, local copies, waits for them, and re-layouts, unpack(): flat[offset:offset + height * breadth].reshape(height, breadth)  23.6 us
    dot_general x1, matrix products, shards(): jnp.dot(normed_two_low, w_in, preferred_element_type=jnp.float32) + bias_in  21.2 us
    dot_general x4, matrix products, contract_cols(): lax.dot_general(left, right, (((1,), (1,)), ((), ())), preferred_element_...  18.7 us
    dot_general x4, matrix products, contract_rows(): lax.dot_general(left, right, (((0,), (0,)), ((), ())), preferred_element_...  15.4 us
  transfers between devices with their start and end apart: 2, of which 2 were waited for; matrix products, arithmetic and copies ran while one was open for 1% of the time, Pallas kernels for 0%

profile of v1, /device:TPU:0, one launch (start us, length us, event | category | flops | bytes accessed | tf_op | source)
XLA Modules:
  0.0 554.7 jit_solution(4443049954293933654)
XLA Ops:
  12.1 104.9 %all-gather.2.cloned.1.call-done = bf16[55552,128]{1,0:T(8,128)(2,1)} async-done(((bf16[1736,128]{1,0:T(8,128)(2,1)}), bf16[55552,128]{1,0:T(8,128)(2,1)}) %all-gather.2.cloned.1.call-update) | async-done | bytes 14221328 | tf_op jit(solution)/shard_map/all_gather | solution.py:48
  122.1 5.2 reshape.209
  127.3 8.3 %fusion.56 = (bf16[18432,128]{1,0:T(8,128)(2,1)}, bf16[18432,128]{1,0:T(8,128)(2,1)}) fusion(bf16[55552,128]{1,0:T(8,128)(2,1)} %all-gather.2.cloned.1.call-done), kind=kLoop, calls=%fused_computation.128 | loop fusion | bytes 18874368 | tf_op jit(solution)/shard_map/slice | solution.py:28
  135.7 8.3 %reshape.213 = bf16[768,3072]{1,0:T(8,128)(2,1)} reshape(bf16[18432,128]{1,0:T(8,128)(2,1)} %get-tuple-element.40) | data formatting | bytes 9437184 | tf_op jit(solution)/shard_map/reshape | solution.py:28
  144.8 4.2 fusion.6
  149.0 6.0 %reshape.210 = bf16[32,16,3,12,64]{4,3,2,1,0:T(8,128)(2,1)} reshape(bf16[512,2304]{1,0:T(8,128)(2,1)S(1)} %fusion.6) | data formatting | bytes 4718592 | tf_op jit(solution)/shard_map/reshape | solution.py:105
  155.0 5.0 fusion.57
  166.0 3.9 convert_element_type.189
  169.9 2.6 fusion.58
  173.9 8.2 %reshape.212 = bf16[768,3072]{1,0:T(8,128)(2,1)} reshape(bf16[18432,128]{1,0:T(8,128)(2,1)} %get-tuple-element.41) | data formatting | bytes 9437184 | tf_op jit(solution)/shard_map/reshape | solution.py:28
  182.8 21.2 %multiply_convert_fusion = (bf16[512,3072]{1,0:T(8,128)(2,1)S(1)}, f32[512,3072]{1,0:T(8,128)}, f32[512,3072]{1,0:T(8,128)}) fusion(f32[3072]{0:T(1024)S(1)} %fusion.30, bf16[768,3072]{1,0:T(8,128)(2,1)} %reshape.212, f32[512,768]{1,0:T(8,128)} %copy-done.12, f32[768]{0:T(1024)S(1)} %get-tuple-element.33, f32[768]{0:T(1024)S(1)} %get-tuple-element.34, ...), kind=kOutput, calls=%fused_computation.4 | convolution fusion | flops 2521694208 | bytes 22042624 | tf_op jit(solution)/shard_map/dot_general | solution.py:122
  204.0 7.7 %multiply_reduce_fusion.4 = (f32[512]{0:T(512)S(1)}, bf16[512,768]{1,0:T(8,128)(2,1)}, f32[512,768]{1,0:T(8,128)}) fusion(bf16[512,768]{1,0:T(8,128)(2,1)S(1)} %copy-done.21, f32[512,768]{1,0:T(8,128)S(1)} %copy-done.13, f32[768]{0:T(1024)S(1)} %get-tuple-element.32, bf16[512,3072]{1,0:T(8,128)(2,1)S(1)} %get-tuple-element.30, bf16[768,3072]{1,0:T(8,128)(2,1)} %reshape.213), kind=kOutput, calls=%fused_computation.58 | convolution fusion | flops 2418671104 | bytes 12588032 | tf_op jit(solution)/shard_map/dot_general | solution.py:66
  212.4 39.0 %all-reduce.1 = (f32[]{:T(128)}, f32[]{:T(128)}) all-reduce(f32[]{:T(128)} %get-tuple-element.16, f32[]{:T(128)} %get-tuple-element.15), channel_id=1, replica_groups=mesh['dp'=8,'fsdp'=4] {'dp','fsdp'}, use_global_device_ids=true, to_apply=%region_8.0 | all-reduce | flops 2 | bytes 16 | tf_op jit(solution)/shard_map/psum | solution.py:128
  252.1 2.6 fusion.53
  254.8 9.9 %fusion.52 = (bf16[3072]{0:T(1024)(128)(2,1)}, bf16[512,3072]{1,0:T(8,128)(2,1)S(1)}) fusion(f32[512,3072]{1,0:T(8,128)} %get-tuple-element.31, f32[512,3072]{1,0:T(8,128)} %get-tuple-element.51, f32[3072]{0:T(1024)S(1)} %fusion.30, bf16[512,768]{1,0:T(8,128)(2,1)S(1)} %get-tuple-element.25, bf16[768,3072]{1,0:T(8,128)(2,1)} %reshape.213), kind=kOutput, calls=%fused_computation.125 | convolution fusion | flops 2441081856 | bytes 21252096 | tf_op jit(solution)/shard_map/dot_general | solution.py:136
  264.6 3.5 multiply_reduce_fusion.2
  268.1 4.9 fusion.11
  279.1 3.9 reshape.214
  283.0 3.9 multiply_reduce_fusion
  293.2 4.3 copy.36
  297.5 7.3 %convert_element_type.211 = bf16[512,2304]{1,0:T(8,128)(2,1)S(1)} reshape(bf16[32,16,3,12,64]{4,3,2,1,0:T(8,128)(2,1)} %copy.36) | data formatting | bytes 4718592 | tf_op jit(solution)/shard_map/convert_element_type | solution.py:173
  304.8 5.8 %fusion.49 = (bf16[768]{0:T(1024)(128)(2,1)}, f32[512]{0:T(512)S(1)}, f32[512,768]{1,0:T(8,128)}) fusion(f32[768]{0:T(1024)S(1)} %get-tuple-element.39, f32[512]{0:T(512)S(1)} %broadcast_multiply_fusion.1, bf16[512,768]{1,0:T(8,128)(2,1)S(1)} %copy-done.9, bf16[512,2304]{1,0:T(8,128)(2,1)S(1)} %convert_element_type.211, bf16[768,2304]{1,0:T(8,128)(2,1)} %reshape.209), kind=kOutput, calls=%fused_computation.124 | convolution fusion | flops 1814297344 | bytes 8266240 | tf_op jit(solution)/shard_map/dot_general | solution.py:66
  311.5 4.0 convolution_convert_fusion.2
  315.5 4.6 fusion.12
  320.1 3.5 copy.42
  325.7 6.4 %reshape.215 = bf16[1769472]{0:T(1024)(128)(2,1)S(1)} reshape(bf16[768,2304]{1,0:T(8,128)(2,1)} %convolution_convert_fusion.2) | data formatting | bytes 7077888 | tf_op jit(solution)/shard_map/reshape | solution.py:184
  332.2 3.8 copy.43
  340.9 2.6 constant_dynamic-update-slice_fusion.2
  343.5 2.6 constant_dynamic-update-slice_fusion.1
  360.1 3.1 add_multiply_fusion
  363.2 179.6 %reduce-scatter.5.cloned.1.call-done = bf16[1736,128]{1,0:T(8,128)(2,1)} async-done(((bf16[55552,128]{1,0:T(8,128)(2,1)}), bf16[1736,128]{1,0:T(8,128)(2,1)}) %reduce-scatter.5.cloned.1.call-update) | async-done | bytes 444432
  542.8 3.5 multiply_subtract_fusion
  (149 shorter events, 52.7 us)
Async XLA Ops:
  7.2 109.9 %all-gather.2.cloned.1.call-start = ((), (), s32[]{:S(2)}) async-start(), calls=%async_computation.1 | async-start | bytes 14665728 | tf_op jit(solution)/shard_map/all_gather | solution.py:48
  9.2 533.6 %reduce-scatter.5.cloned.1.call-start = ((), (), s32[]{:S(2)}) async-start(), calls=%async_computation.2 | async-start | bytes 14665728
  12.1 299.4 %copy-start.26 = (f32[512]{0:T(512)}, f32[512]{0:T(512)S(1)}, u32[]{:S(2)}) copy-start(f32[512]{0:T(512)S(1)} %fusion.39) | copy-start | bytes 6148
  135.7 9.1 %copy-start.8 = (bf16[512,768]{1,0:T(8,128)(2,1)S(1)}, bf16[512,768]{1,0:T(8,128)(2,1)}, u32[]{:S(2)}) copy-start(bf16[512,768]{1,0:T(8,128)(2,1)} %param.6) | copy-start | bytes 2359300
  182.8 21.2 %copy-start.13 = (f32[512,768]{1,0:T(8,128)S(1)}, f32[512,768]{1,0:T(8,128)}, u32[]{:S(2)}) copy-start(f32[512,768]{1,0:T(8,128)} %copy-done.12) | copy-start | bytes 4718596
  182.8 21.2 %copy-start.21 = (bf16[512,768]{1,0:T(8,128)(2,1)S(1)}, bf16[512,768]{1,0:T(8,128)(2,1)}, u32[]{:S(2)}) copy-start(bf16[512,768]{1,0:T(8,128)(2,1)} %param.8) | copy-start | bytes 2359300
  204.0 7.7 %copy-start.37 = (bf16[512,3072]{1,0:T(8,128)(2,1)}, bf16[512,3072]{1,0:T(8,128)(2,1)S(1)}, u32[]{:S(2)}) copy-start(bf16[512,3072]{1,0:T(8,128)(2,1)S(1)} %get-tuple-element.30) | copy-start | bytes 9437188
  204.0 7.7 %copy-start.32 = (s32[512]{0:T(512)S(1)}, s32[512]{0:T(512)}, u32[]{:S(2)}) copy-start(s32[512]{0:T(512)} %param.7) | copy-start | bytes 6148
  252.1 12.5 %slice-start.6 = ((s8[4718592]{0:T(1024)(128)(4,1)}), s8[4194304]{0:T(1024)(128)(4,1)S(1)}, s32[]{:S(2)}) async-start(s8[4718592]{0:T(1024)(128)(4,1)} %bitcast.110), calls=%async_computation.9 | async-start | bytes 8388608
  254.7 9.9 %copy-start.24 = (bf16[512,768]{1,0:T(8,128)(2,1)}, bf16[512,768]{1,0:T(8,128)(2,1)S(1)}, u32[]{:S(2)}) copy-start(bf16[512,768]{1,0:T(8,128)(2,1)S(1)} %get-tuple-element.25) | copy-start | bytes 2359300
  254.7 9.9 %copy-start.14 = (f32[512,768]{1,0:T(8,128)S(1)}, f32[512,768]{1,0:T(8,128)}, u32[]{:S(2)}) copy-start(f32[512,768]{1,0:T(8,128)} %copy-done.12) | copy-start | bytes 4718596
  254.8 9.9 %slice-start.7 = ((s8[4718592]{0:T(1024)(128)(4,1)}), s8[524288]{0:T(1024)(128)(4,1)S(1)}, s32[]{:S(2)}) async-start(s8[4718592]{0:T(1024)(128)(4,1)} %bitcast.110), calls=%async_computation.10 | async-start | bytes 1048576
  283.0 3.9 copy-start.2
  297.5 7.3 %copy-start.9 = (bf16[512,768]{1,0:T(8,128)(2,1)S(1)}, bf16[512,768]{1,0:T(8,128)(2,1)}, u32[]{:S(2)}) copy-start(bf16[512,768]{1,0:T(8,128)(2,1)} %param.6) | copy-start | bytes 2359300
  311.5 4.1 copy-start.25
  311.5 4.1 copy-start.38
  311.5 8.7 %slice-start.4 = ((s8[4718592]{0:T(1024)(128)(4,1)}), s8[4194304]{0:T(1024)(128)(4,1)S(1)}, s32[]{:S(2)}) async-start(s8[4718592]{0:T(1024)(128)(4,1)} %bitcast.108), calls=%async_computation.7 | async-start | bytes 8388608
  315.5 4.6 slice-start.5
  320.1 3.6 copy-start.17
  332.2 5.8 %copy-start.27 = (f32[512]{0:T(512)S(1)}, f32[512]{0:T(512)}, u32[]{:S(2)}) copy-start(f32[512]{0:T(512)} %copy-done.26) | copy-start | bytes 6148
  332.2 8.7 %slice-start = ((s8[4718592]{0:T(1024)(128)(4,1)}), s8[524288]{0:T(1024)(128)(4,1)S(1)}, s32[]{:S(2)}) async-start(s8[4718592]{0:T(1024)(128)(4,1)} %bitcast.104), calls=%async_computation.3 | async-start | bytes 1048576
  336.0 3.7 copy-start.18
  336.0 4.8 slice-start.1
  343.4 4.1 copy-start.36
  343.4 5.5 copy-start.31
  343.4 6.9 %copy-start.30 = (bf16[768]{0:T(1024)(128)(2,1)S(1)}, bf16[768]{0:T(1024)(128)(2,1)}, u32[]{:S(2)}) copy-start(bf16[768]{0:T(1024)(128)(2,1)} %get-tuple-element.10) | copy-start | bytes 4612
  343.5 8.3 %copy-start.29 = (bf16[768]{0:T(1024)(128)(2,1)S(1)}, bf16[768]{0:T(1024)(128)(2,1)}, u32[]{:S(2)}) copy-start(bf16[768]{0:T(1024)(128)(2,1)} %get-tuple-element.26) | copy-start | bytes 4612
  343.5 9.7 %copy-start.35 = (bf16[768]{0:T(1024)(128)(2,1)S(1)}, bf16[768]{0:T(1024)(128)(2,1)}, u32[]{:S(2)}) copy-start(bf16[768]{0:T(1024)(128)(2,1)} %get-tuple-element.6) | copy-start | bytes 4612
  343.5 11.0 %copy-start.34 = (bf16[768]{0:T(1024)(128)(2,1)S(1)}, bf16[768]{0:T(1024)(128)(2,1)}, u32[]{:S(2)}) copy-start(bf16[768]{0:T(1024)(128)(2,1)} %get-tuple-element.12) | copy-start | bytes 4612
  343.5 12.4 %copy-start.28 = (bf16[768]{0:T(1024)(128)(2,1)S(1)}, bf16[768]{0:T(1024)(128)(2,1)}, u32[]{:S(2)}) copy-start(bf16[768]{0:T(1024)(128)(2,1)} %get-tuple-element.24) | copy-start | bytes 4612
  343.5 13.8 %copy-start.33 = (bf16[3072]{0:T(1024)(128)(2,1)S(1)}, bf16[3072]{0:T(1024)(128)(2,1)}, u32[]{:S(2)}) copy-start(bf16[3072]{0:T(1024)(128)(2,1)} %get-tuple-element.22) | copy-start | bytes 18436
  358.5 184.3 %copy-start.19 = (f32[1736,128]{1,0:T(8,128)S(1)}, f32[1736,128]{1,0:T(8,128)}, u32[]{:S(2)}) copy-start(f32[1736,128]{1,0:T(8,128)} %param.9) | copy-start | bytes 2666500
  (17 other events, 30.4 us)
Sparse Core Ops, SparseCore 0:
  11.4 105.5 all-gather.1
  358.6 184.1 reduce-scatter.4
